TPU v7x, 256 devices: a 8x8x2 block of a 8x8x16 slice. The times are simulated.
256 devices in a mesh: grp: 2 (over z), row: 128 (over y, x, core).
Axes of the slice: x: 8, y: 8, z: 2, core: 2. Of those that a mesh axis runs over, the one named last changes fastest.
The devices are a block of a 8x8x16 slice.
Arguments:
- concentration: float32 [16, 1024, 1024], P('grp', 'row'), parts along dimension 0, may hold values from -0.95 to 1.35
- target_mass: float32 [16], P('grp'), parts along dimension 0, may hold values from 0 to 0.4
- mobility: float32 [16], P('grp'), parts along dimension 0, may hold values from 0.5 to 2
Outputs:
- updated: float32 [16, 1024, 1024], P('grp', 'row'), parts along dimension 0
- residual: float32 [16], P('grp'), parts along dimension 0
There are 2 independent parts, one for each index of `grp`. A program takes and returns all parts, laid end to end along the dimension named above; each array names one. Nothing has to cross between parts.
All inputs are finite; a program needn't handle non-finite values.
Results may differ from a plain program's by a relative error of at most 0.00005.
Values sent between devices are 32-bit elements; how exact they have to be, the bound alone decides.
A program may use at most 64 MiB of HBM per device.

v0:
```python
import math
import jax
import jax.numpy as jnp
from jax import lax
from jax.sharding import Mesh
from jax.sharding import PartitionSpec as P

ROW = ("row_0", "row_1", "row_2")
stiffness = 1.0
time_step = 0.05
stabilizer = 2.0


def by_axis(x, axes):
    for axis in axes:
        x = lax.psum(x, axis)
    return x


def make_tables(length):
    blocks = length // 128
    short_range = jnp.arange(blocks, dtype=jnp.int32)
    long_range = jnp.arange(128, dtype=jnp.int32)
    short_angle = (short_range[:, None] * short_range[None, :] % blocks).astype(jnp.float32) * (
        2.0 * math.pi / blocks
    )
    long_angle = (long_range[:, None] * long_range[None, :] % 128).astype(jnp.float32) * (
        2.0 * math.pi / 128
    )
    twist_angle = (short_range[:, None] * long_range[None, :]).astype(jnp.float32) * (
        2.0 * math.pi / length
    )
    return (
        jnp.cos(short_angle),
        jnp.sin(short_angle),
        jnp.cos(long_angle),
        jnp.sin(long_angle),
        jnp.cos(twist_angle),
        jnp.sin(twist_angle),
    )


def product(pattern, real_part, imag_part, cosine, sine, orient, real_only=False):

    def contract(operand, table):
        return jnp.einsum(pattern, operand, table, precision=lax.Precision.HIGHEST)

    if imag_part is None:
        return (contract(real_part, cosine), orient * contract(real_part, sine))
    if real_only:
        return (contract(real_part, cosine) - orient * contract(imag_part, sine), None)
    return (
        contract(real_part, cosine) - orient * contract(imag_part, sine),
        contract(imag_part, cosine) + orient * contract(real_part, sine),
    )


def rotate(real_part, imag_part, tables, orient):
    cosine, sine = (tables[4], tables[5])
    return (
        real_part * cosine - orient * imag_part * sine,
        imag_part * cosine + orient * real_part * sine,
    )


def forward_rows(real_field, tables, imag_field=None):
    planes, narrow, length = real_field.shape
    block_shape = (planes, narrow, length // 128, 128)
    shaped = real_field.reshape(block_shape)
    imag_shaped = None
    real_part, imag_part = product("pxab,ac->pxcb", shaped, imag_shaped, tables[0], tables[1], -1.0)
    real_part, imag_part = rotate(real_part, imag_part, tables, -1.0)
    real_part, imag_part = product(
        "pxcb,bd->pcdx", real_part, imag_part, tables[2], tables[3], -1.0
    )
    return (real_part.reshape(planes, length, narrow), imag_part.reshape(planes, length, narrow))


def forward_cols(pieces, tables):
    real_part, imag_part = pieces
    planes, narrow, length = real_part.shape
    shape = (planes, narrow, length // 128, 128)
    real_part, imag_part = product(
        "pqab,ac->pqcb",
        real_part.reshape(shape),
        imag_part.reshape(shape),
        tables[0],
        tables[1],
        -1.0,
    )
    real_part, imag_part = rotate(real_part, imag_part, tables, -1.0)
    real_part, imag_part = product(
        "pqcb,bd->pqcd", real_part, imag_part, tables[2], tables[3], -1.0
    )
    return (real_part.reshape(planes, narrow, length), imag_part.reshape(planes, narrow, length))


def inverse_cols(real_part, imag_part, tables):
    planes, narrow, length = real_part.shape
    shape = (planes, narrow, length // 128, 128)
    real_part, imag_part = product(
        "pqcd,db->pqcb",
        real_part.reshape(shape),
        imag_part.reshape(shape),
        tables[2],
        tables[3],
        1.0,
    )
    real_part, imag_part = rotate(real_part, imag_part, tables, 1.0)
    real_part, imag_part = product("pqcb,ca->pabq", real_part, imag_part, tables[0], tables[1], 1.0)
    return (real_part.reshape(planes, length, narrow), imag_part.reshape(planes, length, narrow))


def inverse_rows(pieces, tables):
    real_part, imag_part = pieces
    planes, narrow, length = real_part.shape
    shape = (planes, narrow, length // 128, 128)
    real_part, imag_part = product(
        "pxcd,db->pxcb",
        real_part.reshape(shape),
        imag_part.reshape(shape),
        tables[2],
        tables[3],
        1.0,
    )
    real_part, imag_part = rotate(real_part, imag_part, tables, 1.0)
    real_part, imag_part = product(
        "pxcb,ca->pxab", real_part, imag_part, tables[0], tables[1], 1.0, True
    )
    real_part = real_part.reshape(planes, narrow, length)
    return real_part


def digit_natural(positions, length):
    blocks = length // 128
    return positions // 128 + blocks * (positions % 128)


def wavenumbers(natural_index, length):
    signed = jnp.where(natural_index < length // 2, natural_index, natural_index - length)
    angular = signed.astype(jnp.float32) * (2.0 * math.pi / length)
    return (angular, jnp.where(natural_index == length // 2, jnp.float32(0.0), angular))


def local(concentration, target_mass, mobility):
    planes, rows_local, width_y = concentration.shape
    devices = lax.axis_size(ROW)
    width_x = rows_local * devices
    cols_local = width_y // devices
    cells = float(width_x * width_y)
    inverse_cells = 1.0 / cells
    residual = by_axis(jnp.sum(concentration, axis=(1, 2)), ROW) / cells - target_mass
    tables_y = make_tables(width_y)
    device = lax.axis_index(ROW)
    local_slots = jnp.arange(cols_local, dtype=jnp.int32)
    columns = device * cols_local + local_slots
    all_x = jnp.arange(width_x, dtype=jnp.int32)
    natural_x = digit_natural(all_x, width_x)
    angular_x, slope_x = wavenumbers(natural_x, width_x)
    angular_x, slope_x = (angular_x[None, :], slope_x[None, :])
    cubic_term = concentration * concentration * concentration - concentration

    def to_spectrum(pieces):
        return forward_cols(pieces, tables_y)

    angular_y, slope_y = wavenumbers(digit_natural(columns, width_y), width_y)
    stacked = jnp.concatenate([concentration, cubic_term], axis=0)
    half_real, half_imag = forward_rows(stacked, tables_y)
    spec_real, spec_imag = to_spectrum(
        (
            lax.all_to_all(half_real, ROW, split_axis=1, concat_axis=2, tiled=True),
            lax.all_to_all(half_imag, ROW, split_axis=1, concat_axis=2, tiled=True),
        )
    )
    field_real, field_imag = (spec_real[:planes], spec_imag[:planes])
    cubic_real, cubic_imag = (spec_real[planes:], spec_imag[planes:])
    angular_y, slope_y = (angular_y[:, None], slope_y[:, None])
    square = angular_x * angular_x + angular_y * angular_y
    chem_real = (cubic_real + stiffness * square * field_real) * inverse_cells
    chem_imag = (cubic_imag + stiffness * square * field_imag) * inverse_cells
    stack_real = jnp.concatenate([-slope_x * chem_imag, -slope_y * chem_imag], axis=0)
    stack_imag = jnp.concatenate([slope_x * chem_real, slope_y * chem_real], axis=0)
    back_real, back_imag = inverse_cols(stack_real, stack_imag, tables_y)
    gradient_pair = inverse_rows(
        (
            lax.all_to_all(back_real, ROW, split_axis=1, concat_axis=2, tiled=True),
            lax.all_to_all(back_imag, ROW, split_axis=1, concat_axis=2, tiled=True),
        ),
        tables_y,
    )
    grad_x = gradient_pair[:planes]
    grad_y = gradient_pair[planes:]
    weight = mobility[:, None, None] / (1.0 + concentration * concentration)
    fluxes = jnp.concatenate([weight * grad_x, weight * grad_y], axis=0)
    flux_half_real, flux_half_imag = forward_rows(fluxes, tables_y)
    flux_real, flux_imag = to_spectrum(
        (
            lax.all_to_all(flux_half_real, ROW, split_axis=1, concat_axis=2, tiled=True),
            lax.all_to_all(flux_half_imag, ROW, split_axis=1, concat_axis=2, tiled=True),
        )
    )
    flux_x_real, flux_x_imag = (flux_real[:planes], flux_imag[:planes])
    flux_y_real, flux_y_imag = (flux_real[planes:], flux_imag[planes:])
    div_real = -slope_x * flux_x_imag - slope_y * flux_y_imag
    div_imag = slope_x * flux_x_real + slope_y * flux_y_real
    factor = (
        time_step
        * inverse_cells
        / (
            1.0
            + time_step
            * mobility[:, None, None]
            * (stabilizer * square + stiffness * square * square)
        )
    )
    change_real, change_imag = inverse_cols(div_real * factor, div_imag * factor, tables_y)
    change = inverse_rows(
        (
            lax.all_to_all(change_real, ROW, split_axis=1, concat_axis=2, tiled=True),
            lax.all_to_all(change_imag, ROW, split_axis=1, concat_axis=2, tiled=True),
        ),
        tables_y,
    )
    fresh = concentration + change
    return (fresh - residual[:, None, None], residual)


def solution(mesh):
    torus = Mesh(
        mesh.devices.reshape(mesh.shape["grp"], 8, 8, 2), ("grp", "row_0", "row_1", "row_2")
    )
    in_specs = (P("grp", ROW, None), P("grp"), P("grp"))
    out_specs = (P("grp", ROW, None), P("grp"))
    return jax.shard_map(local, mesh=torus, in_specs=in_specs, out_specs=out_specs, check_vma=False)
```

profile of v0, /device:TPU:513, one launch (start us, length us, event | category | flops | bytes accessed | tf_op | source)
XLA Modules:
  0.0 410.4 jit_solution(5268577525299020385)
XLA Ops:
  6.6 2.7 copy.114
  9.3 4.2 %reshape.381 = f32[128,1,1024]{2,1,0:T(1,128)} reshape(f32[1024,8,16]{2,1,0:T(8,128)} %bitcast.296) | data formatting | bytes 1048576
  13.5 28.1 %all-to-all-start.1 = ((f32[128,1,1024]{2,1,0:T(1,128)}), f32[128,1,1024]{2,1,0:T(1,128)S(1)}, u32[]{:S(2)}, u32[]{:S(2)}) async-start(f32[128,1,1024]{2,1,0:T(1,128)} %reshape.381), calls=%async_computation.1 | async-start | bytes 1048576 | tf_op jit(solution)/shard_map/all_to_all | solution.py:171
  43.9 2.7 copy.108
  46.6 4.2 %reshape.383 = f32[128,1,1024]{2,1,0:T(1,128)} reshape(f32[1024,8,16]{2,1,0:T(8,128)} %bitcast.297) | data formatting | bytes 1048576
  50.8 10.3 %all-to-all-done.1 = f32[128,1,1024]{2,1,0:T(1,128)S(1)} async-done(((f32[128,1,1024]{2,1,0:T(1,128)}), f32[128,1,1024]{2,1,0:T(1,128)S(1)}, u32[]{:S(2)}, u32[]{:S(2)}) %all-to-all-start.1) | async-done | bytes 524320 | tf_op jit(solution)/shard_map/all_to_all | solution.py:171
  61.0 7.5 %all-to-all-start = ((f32[128,1,1024]{2,1,0:T(1,128)}), f32[128,1,1024]{2,1,0:T(1,128)S(1)}, u32[]{:S(2)}, u32[]{:S(2)}) async-start(f32[128,1,1024]{2,1,0:T(1,128)} %reshape.383), calls=%async_computation | async-start | bytes 1048576 | tf_op jit(solution)/shard_map/all_to_all | solution.py:172
  71.1 2.8 reshape.382
  73.9 4.4 %copy.115 = f32[16,8,128,8]{0,3,2,1:T(8,128)} copy(f32[16,8,128,8]{0,3,1,2:T(8,128)} %bitcast.302) | data formatting | bytes 1048576 | tf_op jit(solution)/shard_map/all_to_all | solution.py:171
  78.3 2.9 copy.116
  81.8 6.3 %all-to-all-done = f32[128,1,1024]{2,1,0:T(1,128)S(1)} async-done(((f32[128,1,1024]{2,1,0:T(1,128)}), f32[128,1,1024]{2,1,0:T(1,128)S(1)}, u32[]{:S(2)}, u32[]{:S(2)}) %all-to-all-start) | async-done | bytes 524320 | tf_op jit(solution)/shard_map/all_to_all | solution.py:172
  88.1 1.9 reduce
  90.0 2.8 reshape.384
  92.7 4.4 %copy.109 = f32[16,8,128,8]{0,3,2,1:T(8,128)} copy(f32[16,8,128,8]{0,3,1,2:T(8,128)} %bitcast.304) | data formatting | bytes 1048576 | tf_op jit(solution)/shard_map/all_to_all | solution.py:172
  97.2 3.3 copy.110
  110.4 3.1 copy.159
  113.5 4.2 %reshape.387 = f32[128,1,1024]{2,1,0:T(1,128)} reshape(f32[1024,8,16]{2,1,0:T(8,128)} %bitcast.298) | data formatting | bytes 1048576
  117.7 10.1 %all-to-all-start.2 = ((f32[128,1,1024]{2,1,0:T(1,128)}), f32[128,1,1024]{2,1,0:T(1,128)S(1)}, u32[]{:S(2)}, u32[]{:S(2)}) async-start(f32[128,1,1024]{2,1,0:T(1,128)} %reshape.387), calls=%async_computation.2 | async-start | bytes 1048576 | tf_op jit(solution)/shard_map/all_to_all | solution.py:186
  129.0 3.1 copy.160
  132.1 4.2 %reshape.385 = f32[128,1,1024]{2,1,0:T(1,128)} reshape(f32[1024,8,16]{2,1,0:T(8,128)} %bitcast.299) | data formatting | bytes 1048576
  136.3 11.1 %all-to-all-done.2 = f32[128,1,1024]{2,1,0:T(1,128)S(1)} async-done(((f32[128,1,1024]{2,1,0:T(1,128)}), f32[128,1,1024]{2,1,0:T(1,128)S(1)}, u32[]{:S(2)}, u32[]{:S(2)}) %all-to-all-start.2) | async-done | bytes 524320 | tf_op jit(solution)/shard_map/all_to_all | solution.py:186
  147.4 7.5 %all-to-all-start.3 = ((f32[128,1,1024]{2,1,0:T(1,128)}), f32[128,1,1024]{2,1,0:T(1,128)S(1)}, u32[]{:S(2)}, u32[]{:S(2)}) async-start(f32[128,1,1024]{2,1,0:T(1,128)} %reshape.385), calls=%async_computation.3 | async-start | bytes 1048576 | tf_op jit(solution)/shard_map/all_to_all | solution.py:187
  154.9 1.9 reduce.3
  156.8 2.9 reshape.388
  159.8 2.5 copy.120
  162.2 6.7 %fusion.104 = f32[16,8,8,128]{3,0,2,1:T(8,128)S(1)} fusion(f32[16,8,8,128]{0,3,2,1:T(8,128)S(1)} %bitcast.292), kind=kOutput, calls=%fused_computation.167 | convolution fusion | flops 201555968 | bytes 1048576 | tf_op jit(solution)/shard_map/pxcd,db->pxcb/dot_general | solution.py:46
  168.9 6.7 %fusion.128 = f32[16,8,8,128]{3,0,2,1:T(8,128)S(1)} fusion(f32[16,8,8,128]{0,3,2,1:T(8,128)S(1)} %bitcast.293), kind=kOutput, calls=%fused_computation.191 | convolution fusion | flops 201555968 | bytes 1048576 | tf_op jit(solution)/shard_map/pxcd,db->pxcb/dot_general | solution.py:46
  175.6 1.9 reduce.2
  177.5 3.1 reshape.386
  180.7 2.5 copy.123
  183.1 6.7 %fusion.106 = f32[16,8,8,128]{3,0,2,1:T(8,128)S(1)} fusion(f32[16,8,8,128]{0,3,2,1:T(8,128)S(1)} %bitcast.294), kind=kOutput, calls=%fused_computation.169 | convolution fusion | flops 201555968 | bytes 1048576 | tf_op jit(solution)/shard_map/pxcd,db->pxcb/dot_general | solution.py:46
  189.8 6.7 %fusion.126 = f32[16,8,8,128]{3,0,2,1:T(8,128)S(1)} fusion(f32[16,8,8,128]{0,3,2,1:T(8,128)S(1)} %bitcast.295), kind=kOutput, calls=%fused_computation.189 | convolution fusion | flops 201555968 | bytes 1048576 | tf_op jit(solution)/shard_map/pxcd,db->pxcb/dot_general | solution.py:46
  203.8 2.7 copy.140
  206.5 4.2 %reshape.389 = f32[128,1,1024]{2,1,0:T(1,128)} reshape(f32[1024,8,16]{2,1,0:T(8,128)} %bitcast.300) | data formatting | bytes 1048576
  210.7 17.1 %all-to-all-start.5 = ((f32[128,1,1024]{2,1,0:T(1,128)}), f32[128,1,1024]{2,1,0:T(1,128)S(1)}, u32[]{:S(2)}, u32[]{:S(2)}) async-start(f32[128,1,1024]{2,1,0:T(1,128)} %reshape.389), calls=%async_computation.5 | async-start | bytes 1048576 | tf_op jit(solution)/shard_map/all_to_all | solution.py:198
  230.1 2.7 copy.134
  232.9 4.2 %reshape.391 = f32[128,1,1024]{2,1,0:T(1,128)} reshape(f32[1024,8,16]{2,1,0:T(8,128)} %bitcast.301) | data formatting | bytes 1048576
  237.0 9.9 %all-to-all-done.5 = f32[128,1,1024]{2,1,0:T(1,128)S(1)} async-done(((f32[128,1,1024]{2,1,0:T(1,128)}), f32[128,1,1024]{2,1,0:T(1,128)S(1)}, u32[]{:S(2)}, u32[]{:S(2)}) %all-to-all-start.5) | async-done | bytes 524320 | tf_op jit(solution)/shard_map/all_to_all | solution.py:198
  247.0 7.5 %all-to-all-start.4 = ((f32[128,1,1024]{2,1,0:T(1,128)}), f32[128,1,1024]{2,1,0:T(1,128)S(1)}, u32[]{:S(2)}, u32[]{:S(2)}) async-start(f32[128,1,1024]{2,1,0:T(1,128)} %reshape.391), calls=%async_computation.4 | async-start | bytes 1048576 | tf_op jit(solution)/shard_map/all_to_all | solution.py:199
  254.5 1.9 reduce.5
  256.4 2.8 reshape.390
  259.1 4.4 %copy.141 = f32[16,8,128,8]{0,3,2,1:T(8,128)} copy(f32[16,8,128,8]{0,3,1,2:T(8,128)} %bitcast.308) | data formatting | bytes 1048576 | tf_op jit(solution)/shard_map/all_to_all | solution.py:198
  263.6 2.9 copy.142
  267.0 7.0 %all-to-all-done.4 = f32[128,1,1024]{2,1,0:T(1,128)S(1)} async-done(((f32[128,1,1024]{2,1,0:T(1,128)}), f32[128,1,1024]{2,1,0:T(1,128)S(1)}, u32[]{:S(2)}, u32[]{:S(2)}) %all-to-all-start.4) | async-done | bytes 524320 | tf_op jit(solution)/shard_map/all_to_all | solution.py:199
  274.0 1.9 reduce.4
  275.9 2.8 reshape.392
  278.7 4.4 %copy.135 = f32[16,8,128,8]{0,3,2,1:T(8,128)} copy(f32[16,8,128,8]{0,3,1,2:T(8,128)} %bitcast.310) | data formatting | bytes 1048576 | tf_op jit(solution)/shard_map/all_to_all | solution.py:199
  283.1 3.0 copy.136
  294.8 3.1 copy.161
  297.9 4.5 %reshape.395 = f32[128,1,512]{2,1,0:T(1,128)} reshape(f32[1024,8,8]{2,1,0:T(8,128)} %bitcast.312) | data formatting | bytes 524288
  302.4 9.3 %all-to-all-start.6 = ((f32[128,1,512]{2,1,0:T(1,128)}), f32[128,1,512]{2,1,0:T(1,128)S(1)}, u32[]{:S(2)}, u32[]{:S(2)}) async-start(f32[128,1,512]{2,1,0:T(1,128)} %reshape.395), calls=%async_computation.6 | async-start | bytes 524288 | tf_op jit(solution)/shard_map/all_to_all | solution.py:219
  312.5 3.1 copy.164
  315.6 4.5 %reshape.393 = f32[128,1,512]{2,1,0:T(1,128)} reshape(f32[1024,8,8]{2,1,0:T(8,128)} %bitcast.313) | data formatting | bytes 524288
  320.1 5.9 %all-to-all-done.6 = f32[128,1,512]{2,1,0:T(1,128)S(1)} async-done(((f32[128,1,512]{2,1,0:T(1,128)}), f32[128,1,512]{2,1,0:T(1,128)S(1)}, u32[]{:S(2)}, u32[]{:S(2)}) %all-to-all-start.6) | async-done | bytes 262176 | tf_op jit(solution)/shard_map/all_to_all | solution.py:219
  326.0 10.4 %all-to-all-start.7 = ((f32[128,1,512]{2,1,0:T(1,128)}), f32[128,1,512]{2,1,0:T(1,128)S(1)}, u32[]{:S(2)}, u32[]{:S(2)}) async-start(f32[128,1,512]{2,1,0:T(1,128)} %reshape.393), calls=%async_computation.7 | async-start | bytes 524288 | tf_op jit(solution)/shard_map/all_to_all | solution.py:220
  336.4 16.2 %psum.21 = f32[8]{0:T(128)S(1)} all-reduce(f32[8]{0:T(128)S(1)} %get-tuple-element.14), channel_id=1, replica_groups=mesh['grp'=2,'row_0'=8,'row_1'=8,'row_2'=2] {'row_0'}, use_global_device_ids=true, to_apply=%region_1.0 | all-reduce | flops 8 | bytes 64 | tf_op jit(solution)/shard_map/psum | solution.py:16
  352.6 12.9 %psum.22 = f32[8]{0:T(128)S(1)} all-reduce(f32[8]{0:T(128)S(1)} %psum.21), channel_id=1, replica_groups=mesh['grp'=2,'row_0'=8,'row_1'=8,'row_2'=2] {'row_1'}, use_global_device_ids=true, to_apply=%region_2.0 | all-reduce | flops 8 | bytes 64 | tf_op jit(solution)/shard_map/psum | solution.py:16
  365.5 9.7 %psum.23 = f32[8]{0:T(128)S(1)} all-reduce(f32[8]{0:T(128)S(1)} %psum.22), channel_id=1, replica_groups=mesh['grp'=2,'row_0'=8,'row_1'=8,'row_2'=2] {'row_2'}, use_global_device_ids=true, to_apply=%region_3.0 | all-reduce | flops 8 | bytes 64 | tf_op jit(solution)/shard_map/psum | solution.py:16
  376.5 3.6 reshape.396
  380.1 6.6 %copy.147 = f32[8,8,128,8]{3,2,1,0:T(8,128)} copy(f32[8,8,128,8]{3,0,1,2:T(8,128)} %bitcast.314) | data formatting | bytes 524288 | tf_op jit(solution)/shard_map/all_to_all | solution.py:219
  386.7 3.6 reshape.373
  392.2 3.6 reshape.394
  395.8 6.6 %copy.150 = f32[8,8,128,8]{3,2,1,0:T(8,128)} copy(f32[8,8,128,8]{3,0,1,2:T(8,128)} %bitcast.315) | data formatting | bytes 524288 | tf_op jit(solution)/shard_map/all_to_all | solution.py:220
  402.4 3.9 reshape.375
  (91 shorter events, 48.6 us)
Async XLA Ops:
  13.5 47.6 %all-to-all-start.1 = ((f32[128,1,1024]{2,1,0:T(1,128)}), f32[128,1,1024]{2,1,0:T(1,128)S(1)}, u32[]{:S(2)}, u32[]{:S(2)}) async-start(f32[128,1,1024]{2,1,0:T(1,128)} %reshape.381), calls=%async_computation.1 | async-start | bytes 1048576 | tf_op jit(solution)/shard_map/all_to_all | solution.py:171
  61.0 27.1 %all-to-all-start = ((f32[128,1,1024]{2,1,0:T(1,128)}), f32[128,1,1024]{2,1,0:T(1,128)S(1)}, u32[]{:S(2)}, u32[]{:S(2)}) async-start(f32[128,1,1024]{2,1,0:T(1,128)} %reshape.383), calls=%async_computation | async-start | bytes 1048576 | tf_op jit(solution)/shard_map/all_to_all | solution.py:172
  117.7 29.7 %all-to-all-start.2 = ((f32[128,1,1024]{2,1,0:T(1,128)}), f32[128,1,1024]{2,1,0:T(1,128)S(1)}, u32[]{:S(2)}, u32[]{:S(2)}) async-start(f32[128,1,1024]{2,1,0:T(1,128)} %reshape.387), calls=%async_computation.2 | async-start | bytes 1048576 | tf_op jit(solution)/shard_map/all_to_all | solution.py:186
  147.4 28.2 %all-to-all-start.3 = ((f32[128,1,1024]{2,1,0:T(1,128)}), f32[128,1,1024]{2,1,0:T(1,128)S(1)}, u32[]{:S(2)}, u32[]{:S(2)}) async-start(f32[128,1,1024]{2,1,0:T(1,128)} %reshape.385), calls=%async_computation.3 | async-start | bytes 1048576 | tf_op jit(solution)/shard_map/all_to_all | solution.py:187
  196.5 3.4 copy-start
  196.5 3.4 copy-start.1
  210.7 36.3 %all-to-all-start.5 = ((f32[128,1,1024]{2,1,0:T(1,128)}), f32[128,1,1024]{2,1,0:T(1,128)S(1)}, u32[]{:S(2)}, u32[]{:S(2)}) async-start(f32[128,1,1024]{2,1,0:T(1,128)} %reshape.389), calls=%async_computation.5 | async-start | bytes 1048576 | tf_op jit(solution)/shard_map/all_to_all | solution.py:198
  247.0 27.1 %all-to-all-start.4 = ((f32[128,1,1024]{2,1,0:T(1,128)}), f32[128,1,1024]{2,1,0:T(1,128)S(1)}, u32[]{:S(2)}, u32[]{:S(2)}) async-start(f32[128,1,1024]{2,1,0:T(1,128)} %reshape.391), calls=%async_computation.4 | async-start | bytes 1048576 | tf_op jit(solution)/shard_map/all_to_all | solution.py:199
  302.4 23.6 %all-to-all-start.6 = ((f32[128,1,512]{2,1,0:T(1,128)}), f32[128,1,512]{2,1,0:T(1,128)S(1)}, u32[]{:S(2)}, u32[]{:S(2)}) async-start(f32[128,1,512]{2,1,0:T(1,128)} %reshape.395), calls=%async_computation.6 | async-start | bytes 524288 | tf_op jit(solution)/shard_map/all_to_all | solution.py:219
  312.5 62.7 %copy-start.3 = (f32[8]{0:T(128)S(1)}, f32[8]{0:T(128)}, u32[]{:S(2)}) copy-start(f32[8]{0:T(128)} %param.4) | copy-start | bytes 100
  326.0 64.9 %all-to-all-start.7 = ((f32[128,1,512]{2,1,0:T(1,128)}), f32[128,1,512]{2,1,0:T(1,128)S(1)}, u32[]{:S(2)}, u32[]{:S(2)}) async-start(f32[128,1,512]{2,1,0:T(1,128)} %reshape.393), calls=%async_computation.7 | async-start | bytes 524288 | tf_op jit(solution)/shard_map/all_to_all | solution.py:220
  375.2 33.9 %copy-start.2 = (f32[8]{0:T(128)}, f32[8]{0:T(128)S(1)}, u32[]{:S(2)}) copy-start(f32[8]{0:T(128)S(1)} %multiply_subtract_fusion.13) | copy-start | bytes 100
where the time goes:
time: 418 us; the launch traced here: 410 us
  local copies, waits for them, and re-layouts  139 us (33%)
  starting transfers between devices  97.4 us (23%)
  matrix products  65.4 us (16%)
  waiting for transfers between devices  50.5 us (12%)
  blocking collectives  38.8 us (9%)
  other arithmetic  17.4 us (4%)
    dot_general x56, matrix products, contract(): return jnp.einsum(pattern, operand, table, precision=lax.Precision.HIGHEST)  65.4 us
    unnamed x24, local copies, waits for them, and re-layouts  58.3 us
    psum x3, blocking collectives, by_axis(): x = lax.psum(x, axis)  38.8 us
    all_to_all x1, starting transfers between devices, local(): lax.all_to_all(half_real, ROW, split_axis=1, concat_axis=2, tiled=True)  28.1 us
    all_to_all x1, starting transfers between devices, local(): lax.all_to_all(flux_half_real, ROW, split_axis=1, concat_axis=2, tiled=True)  17.1 us
    all_to_all x1, waiting for transfers between devices, local(): lax.all_to_all(back_real, ROW, split_axis=1, concat_axis=2, tiled=True)  11.1 us
    all_to_all x1, starting transfers between devices, local(): lax.all_to_all(change_imag, ROW, split_axis=1, concat_axis=2, tiled=True)  10.4 us
    all_to_all x1, waiting for transfers between devices, local(): lax.all_to_all(half_real, ROW, split_axis=1, concat_axis=2, tiled=True)  10.3 us
  transfers between devices with their start and end apart: 8, of which 6 were waited for; matrix products, arithmetic and copies ran while one was open for 24% of the time, Pallas kernels for 0%

commit v1 on v0

--- a/solution.py
+++ b/solution.py
@@ -13,7 +13,7 @@
 
 def by_axis(x, axes):
     for axis in axes:
-        x = lax.psum(x, axis)
+        x = jnp.sum(lax.all_gather(x, axis), 0)
     return x
 
 

time: 418 us -> 423 us (1.012)
    psum x3 -> x0, blocking collectives: 38.8 us -> none  [by_axis(): x = lax.psum(x, axis)]
    unnamed x0 -> x3, blocking collectives: none -> 38.7 us
    unnamed x24 -> x39, local copies, waits for them, and re-layouts: 58.3 us -> 60.9 us
where the time goes in v1:
time: 423 us; the launch traced here: 415 us
  local copies, waits for them, and re-layouts  142 us (34%)
  starting transfers between devices  97.5 us (23%)
  matrix products  65.4 us (15%)
  waiting for transfers between devices  50.4 us (12%)
  blocking collectives  38.7 us (9%)
  other arithmetic  17.5 us (4%)
    dot_general x56, matrix products, contract(): return jnp.einsum(pattern, operand, table, precision=lax.Precision.HIGHEST)  65.4 us
    unnamed x39, local copies, waits for them, and re-layouts  60.9 us
    unnamed x3, blocking collectives  38.7 us
    all_to_all x1, starting transfers between devices, local(): lax.all_to_all(half_real, ROW, split_axis=1, concat_axis=2, tiled=True)  28.1 us
    all_to_all x1, starting transfers between devices, local(): lax.all_to_all(flux_half_real, ROW, split_axis=1, concat_axis=2, tiled=True)  17.1 us
    all_to_all x1, waiting for transfers between devices, local(): lax.all_to_all(back_real, ROW, split_axis=1, concat_axis=2, tiled=True)  11.1 us
    all_to_all x1, starting transfers between devices, local(): lax.all_to_all(change_imag, ROW, split_axis=1, concat_axis=2, tiled=True)  10.4 us
    all_to_all x1, waiting for transfers between devices, local(): lax.all_to_all(half_real, ROW, split_axis=1, concat_axis=2, tiled=True)  10.3 us
  transfers between devices with their start and end apart: 8, of which 6 were waited for; matrix products, arithmetic and copies ran while one was open for 24% of the time, Pallas kernels for 0%

profile of v1, /device:TPU:513, one launch (start us, length us, event | category | flops | bytes accessed | tf_op | source)
XLA Modules:
  0.0 415.2 jit_solution(14711198104284512524)
XLA Ops:
  6.6 2.7 copy.114
  9.3 4.2 %reshape.399 = f32[128,1,1024]{2,1,0:T(1,128)} reshape(f32[1024,8,16]{2,1,0:T(8,128)} %bitcast.299) | data formatting | bytes 1048576
  13.5 28.1 %all-to-all-start.1 = ((f32[128,1,1024]{2,1,0:T(1,128)}), f32[128,1,1024]{2,1,0:T(1,128)S(1)}, u32[]{:S(2)}, u32[]{:S(2)}) async-start(f32[128,1,1024]{2,1,0:T(1,128)} %reshape.399), calls=%async_computation.1 | async-start | bytes 1048576 | tf_op jit(solution)/shard_map/all_to_all | solution.py:171
  43.9 2.7 copy.108
  46.6 4.2 %reshape.401 = f32[128,1,1024]{2,1,0:T(1,128)} reshape(f32[1024,8,16]{2,1,0:T(8,128)} %bitcast.300) | data formatting | bytes 1048576
  50.8 10.3 %all-to-all-done.1 = f32[128,1,1024]{2,1,0:T(1,128)S(1)} async-done(((f32[128,1,1024]{2,1,0:T(1,128)}), f32[128,1,1024]{2,1,0:T(1,128)S(1)}, u32[]{:S(2)}, u32[]{:S(2)}) %all-to-all-start.1) | async-done | bytes 524320 | tf_op jit(solution)/shard_map/all_to_all | solution.py:171
  61.0 7.5 %all-to-all-start = ((f32[128,1,1024]{2,1,0:T(1,128)}), f32[128,1,1024]{2,1,0:T(1,128)S(1)}, u32[]{:S(2)}, u32[]{:S(2)}) async-start(f32[128,1,1024]{2,1,0:T(1,128)} %reshape.401), calls=%async_computation | async-start | bytes 1048576 | tf_op jit(solution)/shard_map/all_to_all | solution.py:172
  71.1 2.8 reshape.400
  73.9 4.4 %copy.115 = f32[16,8,128,8]{0,3,2,1:T(8,128)} copy(f32[16,8,128,8]{0,3,1,2:T(8,128)} %bitcast.305) | data formatting | bytes 1048576 | tf_op jit(solution)/shard_map/all_to_all | solution.py:171
  78.3 2.9 copy.116
  81.8 6.3 %all-to-all-done = f32[128,1,1024]{2,1,0:T(1,128)S(1)} async-done(((f32[128,1,1024]{2,1,0:T(1,128)}), f32[128,1,1024]{2,1,0:T(1,128)S(1)}, u32[]{:S(2)}, u32[]{:S(2)}) %all-to-all-start) | async-done | bytes 524320 | tf_op jit(solution)/shard_map/all_to_all | solution.py:172
  88.1 1.9 reduce
  90.0 2.8 reshape.402
  92.8 4.4 %copy.109 = f32[16,8,128,8]{0,3,2,1:T(8,128)} copy(f32[16,8,128,8]{0,3,1,2:T(8,128)} %bitcast.307) | data formatting | bytes 1048576 | tf_op jit(solution)/shard_map/all_to_all | solution.py:172
  97.2 3.3 copy.110
  110.4 3.1 copy.159
  113.5 4.2 %reshape.405 = f32[128,1,1024]{2,1,0:T(1,128)} reshape(f32[1024,8,16]{2,1,0:T(8,128)} %bitcast.301) | data formatting | bytes 1048576
  117.7 10.1 %all-to-all-start.2 = ((f32[128,1,1024]{2,1,0:T(1,128)}), f32[128,1,1024]{2,1,0:T(1,128)S(1)}, u32[]{:S(2)}, u32[]{:S(2)}) async-start(f32[128,1,1024]{2,1,0:T(1,128)} %reshape.405), calls=%async_computation.2 | async-start | bytes 1048576 | tf_op jit(solution)/shard_map/all_to_all | solution.py:186
  129.0 3.1 copy.160
  132.1 4.2 %reshape.403 = f32[128,1,1024]{2,1,0:T(1,128)} reshape(f32[1024,8,16]{2,1,0:T(8,128)} %bitcast.302) | data formatting | bytes 1048576
  136.3 11.1 %all-to-all-done.2 = f32[128,1,1024]{2,1,0:T(1,128)S(1)} async-done(((f32[128,1,1024]{2,1,0:T(1,128)}), f32[128,1,1024]{2,1,0:T(1,128)S(1)}, u32[]{:S(2)}, u32[]{:S(2)}) %all-to-all-start.2) | async-done | bytes 524320 | tf_op jit(solution)/shard_map/all_to_all | solution.py:186
  147.4 7.5 %all-to-all-start.3 = ((f32[128,1,1024]{2,1,0:T(1,128)}), f32[128,1,1024]{2,1,0:T(1,128)S(1)}, u32[]{:S(2)}, u32[]{:S(2)}) async-start(f32[128,1,1024]{2,1,0:T(1,128)} %reshape.403), calls=%async_computation.3 | async-start | bytes 1048576 | tf_op jit(solution)/shard_map/all_to_all | solution.py:187
  154.9 1.9 reduce.3
  156.8 2.9 reshape.406
  159.8 2.5 copy.120
  162.2 6.7 %fusion.104 = f32[16,8,8,128]{3,0,2,1:T(8,128)S(1)} fusion(f32[16,8,8,128]{0,3,2,1:T(8,128)S(1)} %bitcast.295), kind=kOutput, calls=%fused_computation.167 | convolution fusion | flops 201555968 | bytes 1048576 | tf_op jit(solution)/shard_map/pxcd,db->pxcb/dot_general | solution.py:46
  168.9 6.7 %fusion.128 = f32[16,8,8,128]{3,0,2,1:T(8,128)S(1)} fusion(f32[16,8,8,128]{0,3,2,1:T(8,128)S(1)} %bitcast.296), kind=kOutput, calls=%fused_computation.191 | convolution fusion | flops 201555968 | bytes 1048576 | tf_op jit(solution)/shard_map/pxcd,db->pxcb/dot_general | solution.py:46
  175.6 1.9 reduce.2
  177.5 3.1 reshape.404
  180.7 2.5 copy.123
  183.1 6.7 %fusion.106 = f32[16,8,8,128]{3,0,2,1:T(8,128)S(1)} fusion(f32[16,8,8,128]{0,3,2,1:T(8,128)S(1)} %bitcast.297), kind=kOutput, calls=%fused_computation.169 | convolution fusion | flops 201555968 | bytes 1048576 | tf_op jit(solution)/shard_map/pxcd,db->pxcb/dot_general | solution.py:46
  189.8 6.7 %fusion.126 = f32[16,8,8,128]{3,0,2,1:T(8,128)S(1)} fusion(f32[16,8,8,128]{0,3,2,1:T(8,128)S(1)} %bitcast.298), kind=kOutput, calls=%fused_computation.189 | convolution fusion | flops 201555968 | bytes 1048576 | tf_op jit(solution)/shard_map/pxcd,db->pxcb/dot_general | solution.py:46
  203.8 2.7 copy.140
  206.5 4.2 %reshape.407 = f32[128,1,1024]{2,1,0:T(1,128)} reshape(f32[1024,8,16]{2,1,0:T(8,128)} %bitcast.303) | data formatting | bytes 1048576
  210.7 17.1 %all-to-all-start.5 = ((f32[128,1,1024]{2,1,0:T(1,128)}), f32[128,1,1024]{2,1,0:T(1,128)S(1)}, u32[]{:S(2)}, u32[]{:S(2)}) async-start(f32[128,1,1024]{2,1,0:T(1,128)} %reshape.407), calls=%async_computation.5 | async-start | bytes 1048576 | tf_op jit(solution)/shard_map/all_to_all | solution.py:198
  230.2 2.7 copy.134
  232.9 4.2 %reshape.409 = f32[128,1,1024]{2,1,0:T(1,128)} reshape(f32[1024,8,16]{2,1,0:T(8,128)} %bitcast.304) | data formatting | bytes 1048576
  237.0 9.9 %all-to-all-done.5 = f32[128,1,1024]{2,1,0:T(1,128)S(1)} async-done(((f32[128,1,1024]{2,1,0:T(1,128)}), f32[128,1,1024]{2,1,0:T(1,128)S(1)}, u32[]{:S(2)}, u32[]{:S(2)}) %all-to-all-start.5) | async-done | bytes 524320 | tf_op jit(solution)/shard_map/all_to_all | solution.py:198
  247.0 7.5 %all-to-all-start.4 = ((f32[128,1,1024]{2,1,0:T(1,128)}), f32[128,1,1024]{2,1,0:T(1,128)S(1)}, u32[]{:S(2)}, u32[]{:S(2)}) async-start(f32[128,1,1024]{2,1,0:T(1,128)} %reshape.409), calls=%async_computation.4 | async-start | bytes 1048576 | tf_op jit(solution)/shard_map/all_to_all | solution.py:199
  254.5 1.9 reduce.5
  256.4 2.8 reshape.408
  259.1 4.4 %copy.141 = f32[16,8,128,8]{0,3,2,1:T(8,128)} copy(f32[16,8,128,8]{0,3,1,2:T(8,128)} %bitcast.311) | data formatting | bytes 1048576 | tf_op jit(solution)/shard_map/all_to_all | solution.py:198
  263.6 2.9 copy.142
  267.1 7.0 %all-to-all-done.4 = f32[128,1,1024]{2,1,0:T(1,128)S(1)} async-done(((f32[128,1,1024]{2,1,0:T(1,128)}), f32[128,1,1024]{2,1,0:T(1,128)S(1)}, u32[]{:S(2)}, u32[]{:S(2)}) %all-to-all-start.4) | async-done | bytes 524320 | tf_op jit(solution)/shard_map/all_to_all | solution.py:199
  274.0 1.9 reduce.4
  275.9 2.8 reshape.410
  278.7 4.4 %copy.135 = f32[16,8,128,8]{0,3,2,1:T(8,128)} copy(f32[16,8,128,8]{0,3,1,2:T(8,128)} %bitcast.313) | data formatting | bytes 1048576 | tf_op jit(solution)/shard_map/all_to_all | solution.py:199
  283.1 3.0 copy.136
  294.9 3.1 copy.161
  297.9 4.5 %reshape.413 = f32[128,1,512]{2,1,0:T(1,128)} reshape(f32[1024,8,8]{2,1,0:T(8,128)} %bitcast.315) | data formatting | bytes 524288
  302.4 9.3 %all-to-all-start.6 = ((f32[128,1,512]{2,1,0:T(1,128)}), f32[128,1,512]{2,1,0:T(1,128)S(1)}, u32[]{:S(2)}, u32[]{:S(2)}) async-start(f32[128,1,512]{2,1,0:T(1,128)} %reshape.413), calls=%async_computation.6 | async-start | bytes 524288 | tf_op jit(solution)/shard_map/all_to_all | solution.py:219
  312.6 3.1 copy.164
  315.7 4.5 %reshape.411 = f32[128,1,512]{2,1,0:T(1,128)} reshape(f32[1024,8,8]{2,1,0:T(8,128)} %bitcast.316) | data formatting | bytes 524288
  320.2 5.9 %all-to-all-done.6 = f32[128,1,512]{2,1,0:T(1,128)S(1)} async-done(((f32[128,1,512]{2,1,0:T(1,128)}), f32[128,1,512]{2,1,0:T(1,128)S(1)}, u32[]{:S(2)}, u32[]{:S(2)}) %all-to-all-start.6) | async-done | bytes 262176 | tf_op jit(solution)/shard_map/all_to_all | solution.py:219
  326.0 10.4 %all-to-all-start.7 = ((f32[128,1,512]{2,1,0:T(1,128)}), f32[128,1,512]{2,1,0:T(1,128)S(1)}, u32[]{:S(2)}, u32[]{:S(2)}) async-start(f32[128,1,512]{2,1,0:T(1,128)} %reshape.411), calls=%async_computation.7 | async-start | bytes 524288 | tf_op jit(solution)/shard_map/all_to_all | solution.py:220
  338.0 15.7 %all-reduce = f32[64]{0:T(128)S(1)} all-reduce(f32[64]{0:T(128)S(1)} %dynamic-update-slice), channel_id=2, replica_groups=mesh['grp'=2,'row_0'=8,'row_1'=8,'row_2'=2] {'row_0'}, use_global_device_ids=true, to_apply=%add | all-reduce | flops 64 | bytes 512
  355.3 13.2 %all-reduce.1 = f32[64]{0:T(128)S(1)} all-reduce(f32[64]{0:T(128)S(1)} %dynamic-update-slice.1), channel_id=3, replica_groups=mesh['grp'=2,'row_0'=8,'row_1'=8,'row_2'=2] {'row_1'}, use_global_device_ids=true, to_apply=%add.1 | all-reduce | flops 64 | bytes 512
  370.0 9.8 %all-reduce.2 = f32[16]{0:T(128)S(1)} all-reduce(f32[16]{0:T(128)S(1)} %dynamic-update-slice.2), channel_id=4, replica_groups=mesh['grp'=2,'row_0'=8,'row_1'=8,'row_2'=2] {'row_2'}, use_global_device_ids=true, to_apply=%add.2 | all-reduce | flops 16 | bytes 128
  381.2 3.6 reshape.414
  384.8 6.6 %copy.147 = f32[8,8,128,8]{3,2,1,0:T(8,128)} copy(f32[8,8,128,8]{3,0,1,2:T(8,128)} %bitcast.317) | data formatting | bytes 524288 | tf_op jit(solution)/shard_map/all_to_all | solution.py:219
  391.4 3.6 reshape.373
  397.0 3.6 reshape.412
  400.6 6.6 %copy.150 = f32[8,8,128,8]{3,2,1,0:T(8,128)} copy(f32[8,8,128,8]{3,0,1,2:T(8,128)} %bitcast.318) | data formatting | bytes 524288 | tf_op jit(solution)/shard_map/all_to_all | solution.py:220
  407.2 3.9 reshape.375
  (112 shorter events, 51.4 us)
Async XLA Ops:
  13.5 47.6 %all-to-all-start.1 = ((f32[128,1,1024]{2,1,0:T(1,128)}), f32[128,1,1024]{2,1,0:T(1,128)S(1)}, u32[]{:S(2)}, u32[]{:S(2)}) async-start(f32[128,1,1024]{2,1,0:T(1,128)} %reshape.399), calls=%async_computation.1 | async-start | bytes 1048576 | tf_op jit(solution)/shard_map/all_to_all | solution.py:171
  61.0 27.1 %all-to-all-start = ((f32[128,1,1024]{2,1,0:T(1,128)}), f32[128,1,1024]{2,1,0:T(1,128)S(1)}, u32[]{:S(2)}, u32[]{:S(2)}) async-start(f32[128,1,1024]{2,1,0:T(1,128)} %reshape.401), calls=%async_computation | async-start | bytes 1048576 | tf_op jit(solution)/shard_map/all_to_all | solution.py:172
  117.7 29.7 %all-to-all-start.2 = ((f32[128,1,1024]{2,1,0:T(1,128)}), f32[128,1,1024]{2,1,0:T(1,128)S(1)}, u32[]{:S(2)}, u32[]{:S(2)}) async-start(f32[128,1,1024]{2,1,0:T(1,128)} %reshape.405), calls=%async_computation.2 | async-start | bytes 1048576 | tf_op jit(solution)/shard_map/all_to_all | solution.py:186
  147.4 28.2 %all-to-all-start.3 = ((f32[128,1,1024]{2,1,0:T(1,128)}), f32[128,1,1024]{2,1,0:T(1,128)S(1)}, u32[]{:S(2)}, u32[]{:S(2)}) async-start(f32[128,1,1024]{2,1,0:T(1,128)} %reshape.403), calls=%async_computation.3 | async-start | bytes 1048576 | tf_op jit(solution)/shard_map/all_to_all | solution.py:187
  196.5 3.4 copy-start
  196.5 3.4 copy-start.1
  210.7 36.3 %all-to-all-start.5 = ((f32[128,1,1024]{2,1,0:T(1,128)}), f32[128,1,1024]{2,1,0:T(1,128)S(1)}, u32[]{:S(2)}, u32[]{:S(2)}) async-start(f32[128,1,1024]{2,1,0:T(1,128)} %reshape.407), calls=%async_computation.5 | async-start | bytes 1048576 | tf_op jit(solution)/shard_map/all_to_all | solution.py:198
  247.0 27.1 %all-to-all-start.4 = ((f32[128,1,1024]{2,1,0:T(1,128)}), f32[128,1,1024]{2,1,0:T(1,128)S(1)}, u32[]{:S(2)}, u32[]{:S(2)}) async-start(f32[128,1,1024]{2,1,0:T(1,128)} %reshape.409), calls=%async_computation.4 | async-start | bytes 1048576 | tf_op jit(solution)/shard_map/all_to_all | solution.py:199
  302.4 23.6 %all-to-all-start.6 = ((f32[128,1,512]{2,1,0:T(1,128)}), f32[128,1,512]{2,1,0:T(1,128)S(1)}, u32[]{:S(2)}, u32[]{:S(2)}) async-start(f32[128,1,512]{2,1,0:T(1,128)} %reshape.413), calls=%async_computation.6 | async-start | bytes 524288 | tf_op jit(solution)/shard_map/all_to_all | solution.py:219
  312.5 23.9 %copy-start.6 = (u32[256]{0:T(256)S(1)}, u32[256]{0:T(256)}, u32[]{:S(2)}) copy-start(u32[256]{0:T(256)} %constant.147) | copy-start | bytes 3076
  312.6 41.2 %copy-start.5 = (u32[256]{0:T(256)S(1)}, u32[256]{0:T(256)}, u32[]{:S(2)}) copy-start(u32[256]{0:T(256)} %constant.152) | copy-start | bytes 3076
  312.6 55.9 %copy-start.4 = (u32[256]{0:T(256)S(1)}, u32[256]{0:T(256)}, u32[]{:S(2)}) copy-start(u32[256]{0:T(256)} %constant.157) | copy-start | bytes 3076
  312.6 67.4 %copy-start.3 = (f32[8]{0:T(128)S(1)}, f32[8]{0:T(128)}, u32[]{:S(2)}) copy-start(f32[8]{0:T(128)} %param.4) | copy-start | bytes 100
  326.0 69.7 %all-to-all-start.7 = ((f32[128,1,512]{2,1,0:T(1,128)}), f32[128,1,512]{2,1,0:T(1,128)S(1)}, u32[]{:S(2)}, u32[]{:S(2)}) async-start(f32[128,1,512]{2,1,0:T(1,128)} %reshape.411), calls=%async_computation.7 | async-start | bytes 524288 | tf_op jit(solution)/shard_map/all_to_all | solution.py:220
  380.0 33.9 %copy-start.2 = (f32[8]{0:T(128)}, f32[8]{0:T(128)S(1)}, u32[]{:S(2)}) copy-start(f32[8]{0:T(128)S(1)} %multiply_subtract_fusion.13) | copy-start | bytes 100
